TPU v7x, 32 devices: a whole 2x2x4 slice. The times are simulated.
32 devices in a mesh: ta: 1, gx: 8 (over y, x, core), gy: 4 (over z).
Axes of the slice: x: 2, y: 2, z: 4, core: 2. Of those that a mesh axis runs over, the one named last changes fastest.
Arguments:
- propagator: bfloat16 [1, 2, 4, 3, 4, 3, 64, 4096], P('ta', None, None, None, None, None, 'gx', 'gy'), may hold values from -1.5 to 1.5
- gamma_table: int32 [16, 8], replicated, may hold values from 0 to 3, as said below
Outputs:
- spectrum: float32 [1, 16, 64, 64, 128], P('ta', None, ('gx', 'gy'))
Inputs may be any that keep to these rules, and one draw needn't show every extreme that they name: gamma_table[g, 0:4] is a permutation of 0 to 3, gamma_table[g, 4:8] are powers of i.
All inputs are finite; a program needn't handle non-finite values.
Results may differ from a plain program's by a relative error of at most 0.0061.
Values may be sent and summed in bfloat16 or wider, within the bound.
A program may use at most 192 MiB of HBM per device.

v0:
```python
import math

import jax
import jax.numpy as jnp
from jax import lax
from jax.sharding import PartitionSpec as P

EXTENT = 64


def channel_weights(channel_table):
    spin_index = jnp.arange(4, dtype=jnp.int32)
    targets = channel_table[:, :4]
    codes_all = channel_table[:, 4:]
    mapping = (targets[:, :, None] == spin_index[None, None, :]).astype(jnp.float32)
    phase_real = (codes_all == 0).astype(jnp.float32) - (codes_all == 2).astype(jnp.float32)
    phase_imag = (codes_all == 1).astype(jnp.float32) - (codes_all == 3).astype(jnp.float32)
    pair_real = (
        phase_real[:, None, :] * phase_real[:, :, None]
        - phase_imag[:, None, :] * phase_imag[:, :, None]
    )
    pair_imag = (
        phase_real[:, None, :] * phase_imag[:, :, None]
        + phase_imag[:, None, :] * phase_real[:, :, None]
    )
    source_map = jnp.transpose(mapping, (0, 2, 1))
    selector = source_map[:, :, None, :, None] * mapping[:, None, :, None, :]
    count_channels = channel_table.shape[0]
    weight_real = (pair_real[:, None, :, :, None] * selector).reshape(count_channels, 256)
    weight_imag = (pair_imag[:, None, :, :, None] * selector).reshape(count_channels, 256)
    return (weight_real, weight_imag)


def spin_products(field_real, field_imag):
    site_count = field_real.shape[-1]
    total_real = jnp.zeros((4, 4, 4, 4, site_count), jnp.float32)
    total_imag = jnp.zeros((4, 4, 4, 4, site_count), jnp.float32)
    for color_in in range(3):
        for color_out in range(3):
            left_real = field_real[:, color_in, :, color_out].astype(jnp.float32)
            left_imag = field_imag[:, color_in, :, color_out].astype(jnp.float32)
            total_real = (
                total_real
                + left_real[:, :, None, None] * left_real[None, None]
                + left_imag[:, :, None, None] * left_imag[None, None]
            )
            total_imag = (
                total_imag
                + left_imag[:, :, None, None] * left_real[None, None]
                - left_real[:, :, None, None] * left_imag[None, None]
            )
    return (total_real.reshape(256, site_count), total_imag.reshape(256, site_count))


def dft_tables(length):
    steps_index = lax.iota(jnp.int32, length)
    phases = steps_index[:, None] * steps_index[None, :] % length
    angles = phases.astype(jnp.float32) * (2.0 * math.pi / length)
    norm_factor = 1.0 / math.sqrt(length)
    return (
        (jnp.cos(angles) * norm_factor).astype(jnp.bfloat16),
        (jnp.sin(angles) * norm_factor).astype(jnp.bfloat16),
    )


def transform(complex_pair, which_axis, out_type, cosine, sine_table):
    field_real, field_imag = complex_pair

    def contract_axis(values, weights):
        moved = jnp.tensordot(
            values, weights, axes=([which_axis], [0]), preferred_element_type=jnp.float32
        )
        return jnp.moveaxis(moved, -1, which_axis)

    new_real = contract_axis(field_real, cosine) + contract_axis(field_imag, sine_table)
    new_imag = contract_axis(field_imag, cosine) - contract_axis(field_real, sine_table)
    return (new_real.astype(out_type), new_imag.astype(out_type))


def body(propagator, gamma_table):
    weight_real, weight_imag = channel_weights(gamma_table)
    stack_real = jnp.concatenate([weight_real, -weight_imag], axis=1).astype(jnp.bfloat16)
    stack_imag = jnp.concatenate([weight_imag, weight_real], axis=1).astype(jnp.bfloat16)
    rows_x = propagator.shape[-2]
    cols_yz = propagator.shape[-1]
    rows_y = cols_yz // EXTENT
    site_count = rows_x * cols_yz
    grid_x = lax.axis_size("gx")
    grid_y = lax.axis_size("gy")
    cosine, sine_table = dft_tables(EXTENT)

    def one_slice(slice_block):
        flattened = slice_block.reshape(2, 4, 3, 4, 3, site_count)
        prod_real, prod_imag = spin_products(flattened[0], flattened[1])
        prod_stack = jnp.concatenate([prod_real, prod_imag], axis=0).astype(jnp.bfloat16)
        dens_real = jnp.dot(stack_real, prod_stack, preferred_element_type=jnp.float32).astype(
            jnp.bfloat16
        )
        dens_imag = jnp.dot(stack_imag, prod_stack, preferred_element_type=jnp.float32).astype(
            jnp.bfloat16
        )
        view = (dens_real.shape[0], rows_x * rows_y, EXTENT)
        dens_real = dens_real.reshape(view)
        dens_imag = dens_imag.reshape(view)

        def along(values, weights):
            return jnp.einsum("cpz,zk->ckp", values, weights, preferred_element_type=jnp.float32)

        new_real = along(dens_real, cosine) + along(dens_imag, sine_table)
        new_imag = along(dens_imag, cosine) - along(dens_real, sine_table)
        return (new_real.astype(jnp.bfloat16), new_imag.astype(jnp.bfloat16))

    along_z = lax.map(one_slice, propagator)

    def arrange(values):
        shape_in = values.shape
        values = values.reshape(
            shape_in[0], shape_in[1], shape_in[2], grid_x, grid_y, rows_x, rows_y
        )
        values = jnp.transpose(values, (0, 1, 2, 3, 5, 4, 6))
        return values.reshape(shape_in[0], shape_in[1], shape_in[2], EXTENT, EXTENT)

    arranged = (
        arrange(lax.all_to_all(along_z[0], ("gx", "gy"), split_axis=2, concat_axis=3, tiled=True)),
        arrange(lax.all_to_all(along_z[1], ("gx", "gy"), split_axis=2, concat_axis=3, tiled=True)),
    )
    arranged = transform(arranged, 4, jnp.bfloat16, cosine, sine_table)
    spec_real, spec_imag = transform(arranged, 3, jnp.float32, cosine, sine_table)
    return jnp.concatenate([spec_real, spec_imag], axis=4)


def solution(mesh):
    return jax.shard_map(
        body,
        mesh=mesh,
        in_specs=(P("ta", None, None, None, None, None, "gx", "gy"), P()),
        out_specs=P("ta", None, ("gx", "gy"), None, None),
        check_vma=False,
    )
```

profile of v0, /device:TPU:0, one launch (start us, length us, event | category | flops | bytes accessed | tf_op | source)
XLA Modules:
  0.0 208.0 jit_solution(4332045447886033136)
XLA Ops:
  0.7 4.4 %fusion.124 = (bf16[1,1,4,3,4,3,8,1024]{7,6,5,4,3,2,1,0:T(8,128)(2,1)S(1)}, bf16[1,1,4,3,4,3,8,1024]{7,6,5,4,3,2,1,0:T(8,128)(2,1)}) fusion(bf16[1,2,4,3,4,3,8,1024]{7,6,5,4,3,2,1,0:T(8,128)(2,1)} %param.2), kind=kLoop, calls=%fused_computation.175 | loop fusion | bytes 9437184 | tf_op jit(solution)/shard_map/while/body/eval_jaxpr/slice | solution.py:94
  5.1 1.6 copy.49
  6.7 5.1 %squeeze.47 = bf16[4,3,4,3,8192]{4,2,3,1,0:T(4,128)(2,1)S(1)} reshape(bf16[1,1,4,3,4,3,8,1024]{7,6,4,5,3,2,1,0:T(8,128)(2,1)} %copy.49) | data formatting | bytes 4718592 | tf_op jit(solution)/shard_map/while/body/eval_jaxpr/squeeze | solution.py:94
  11.8 3.4 %copy.50 = bf16[1,1,4,3,4,3,8,1024]{7,6,4,5,3,2,1,0:T(8,128)(2,1)} copy(bf16[1,1,4,3,4,3,8,1024]{7,6,5,4,3,2,1,0:T(8,128)(2,1)} %get-tuple-element.22) | data formatting | bytes 4718592 | tf_op jit(solution)/shard_map/while/body/eval_jaxpr/slice | solution.py:94
  15.2 6.2 %squeeze.48 = bf16[4,3,4,3,8192]{4,2,3,1,0:T(4,128)(2,1)} reshape(bf16[1,1,4,3,4,3,8,1024]{7,6,4,5,3,2,1,0:T(8,128)(2,1)} %copy.50) | data formatting | bytes 4718592 | tf_op jit(solution)/shard_map/while/body/eval_jaxpr/squeeze | solution.py:94
  21.3 2.5 %fusion.24 = (f32[4,4,8192]{2,1,0:T(4,128)S(1)}, f32[4,4,8192]{2,1,0:T(4,128)S(1)}, f32[4,4,8192]{2,1,0:T(4,128)S(1)}, f32[4,4,8192]{2,1,0:T(4,128)S(1)}, f32[4,...) fusion(bf16[4,3,4,3,8192]{4,2,3,1,0:T(4,128)(2,1)} %squeeze.48,, ...), kind=kLoop, calls=%fused_computation.59 | loop fusion | flops 2359296 | bytes 14155776 | tf_op jit(solution)/shard_map/while/body/eval_jaxpr/convert_element_type | solution.py:41
  23.9 37.5 %add_add_fusion = (f32[4,4,4,4,8192]{4,3,2,1,0:T(4,128)}, f32[4,4,4,4,8192]{4,3,2,1,0:T(4,128)}) fusion(f32[4,4,8192]{2,1,0:T(4,128)S(1)} %get-tuple-element.44, f32[4,4,8192]{2,1,0:T(4,128)S(1)} %get-tuple-element.70, f32[4,4,8192]{2,1,0:T(4,128)S(1)} %get-tuple-element.45, f32[4,4,8192]{2,1,0:T(4,128)S(1)} %get-tuple-element.69, ...), kind=kLoop, calls=%fused_computation.4 | loop fusion | flops 130023424 | bytes 25165824 | tf_op jit(solution)/shard_map/while/body/eval_jaxpr/add | solution.py:43
  61.4 10.0 %reshape.473 = f32[256,8192]{1,0:T(8,128)} reshape(f32[4,4,4,4,8192]{4,3,2,1,0:T(4,128)} %get-tuple-element.19) | data formatting | bytes 16777216 | tf_op jit(solution)/shard_map/while/body/eval_jaxpr/add | solution.py:43
  71.5 12.5 %broadcast_multiply_fusion.2 = (f32[4,4,4,4,8192]{4,3,2,1,0:T(4,128)}, f32[4,4,4,4,8192]{4,3,2,1,0:T(4,128)}, f32[4,4,4,4,8192]{4,3,2,1,0:T(4,128)}, f32[4,4,4,4,8192]{4,3,2,1,0:T(4,128)}) fusion(f32[4,4,8192]{2,1,0:T(4,128)S(1)} %get-tuple-element.43, f32[4,4,8192]{2,1,0:T(4,128)S(1)} %get-tuple-element.71), kind=kLoop, calls=%fused_computation.9 | loop fusion | flops 8388608 | bytes 34603008 | tf_op jit(solution)/shard_map/while/body/eval_jaxpr/mul | solution.py:49
  83.9 10.0 %mul.987 = f32[256,8192]{1,0:T(8,128)} reshape(f32[4,4,4,4,8192]{4,3,2,1,0:T(4,128)} %get-tuple-element.53) | data formatting | bytes 16777216 | tf_op jit(solution)/shard_map/while/body/eval_jaxpr/mul | solution.py:44
  93.9 10.0 %mul.991 = f32[256,8192]{1,0:T(8,128)} reshape(f32[4,4,4,4,8192]{4,3,2,1,0:T(4,128)} %get-tuple-element.54) | data formatting | bytes 16777216 | tf_op jit(solution)/shard_map/while/body/eval_jaxpr/mul | solution.py:45
  103.9 10.0 %reshape.474 = f32[256,8192]{1,0:T(8,128)} reshape(f32[4,4,4,4,8192]{4,3,2,1,0:T(4,128)} %get-tuple-element.20) | data formatting | bytes 16777216 | tf_op jit(solution)/shard_map/while/body/eval_jaxpr/sub | solution.py:48
  113.9 10.0 %mul.1021 = f32[256,8192]{1,0:T(8,128)} reshape(f32[4,4,4,4,8192]{4,3,2,1,0:T(4,128)} %get-tuple-element.51) | data formatting | bytes 16777216 | tf_op jit(solution)/shard_map/while/body/eval_jaxpr/mul | solution.py:49
  124.0 10.0 %mul.1023 = f32[256,8192]{1,0:T(8,128)} reshape(f32[4,4,4,4,8192]{4,3,2,1,0:T(4,128)} %get-tuple-element.52) | data formatting | bytes 16777216 | tf_op jit(solution)/shard_map/while/body/eval_jaxpr/mul | solution.py:50
  134.3 9.1 %add_convert_fusion = bf16[256,8192]{1,0:T(8,128)(2,1)S(1)} fusion(f32[256,8192]{1,0:T(8,128)} %mul.991, f32[256,8192]{1,0:T(8,128)} %reshape.473, f32[256,8192]{1,0:T(8,128)} %mul.987), kind=kLoop, calls=%fused_computation.6 | loop fusion | flops 6291456 | bytes 29360128 | tf_op jit(solution)/shard_map/convert.20
  143.4 1.5 copy-done
  144.9 2.4 %copy-done.1 = f32[256,8192]{1,0:T(8,128)S(1)} copy-done((f32[256,8192]{1,0:T(8,128)S(1)}, f32[256,8192]{1,0:T(8,128)}, u32[]{:S(2)}) %copy-start.1) | copy-done | bytes 8388632
  147.3 7.1 %subtract_convert_fusion = bf16[256,8192]{1,0:T(8,128)(2,1)} fusion(f32[256,8192]{1,0:T(8,128)S(1)} %copy-done.1, f32[256,8192]{1,0:T(8,128)} %reshape.474, f32[256,8192]{1,0:T(8,128)S(1)} %copy-done), kind=kLoop, calls=%fused_computation.5 | loop fusion | flops 6291456 | bytes 29360128 | tf_op jit(solution)/shard_map/convert.21
  154.4 4.0 %convolution_convert_fusion.1 = bf16[16,8192]{1,0:T(8,128)(2,1)S(1)} fusion(bf16[256,8192]{1,0:T(8,128)(2,1)} %subtract_convert_fusion, bf16[256,8192]{1,0:T(8,128)(2,1)S(1)} %add_convert_fusion, bf16[16,256]{1,0:T(8,128)(2,1)S(1)} %copy.48, bf16[16,256]{1,0:T(8,128)(2,1)S(1)} %copy.47), kind=kOutput, calls=%fused_computation.1 | convolution fusion | flops 151158784 | bytes 8667136 | tf_op jit(solution)/shard_map/while/body/eval_jaxpr/dot_general | solution.py:96
  159.4 4.7 %convolution_convert_fusion = bf16[16,8192]{1,0:T(8,128)(2,1)S(1)} fusion(bf16[256,8192]{1,0:T(8,128)(2,1)} %subtract_convert_fusion, bf16[256,8192]{1,0:T(8,128)(2,1)} %copy-done.2, bf16[16,256]{1,0:T(8,128)(2,1)S(1)} %copy.47, bf16[16,256]{1,0:T(8,128)(2,1)S(1)} %copy.52), kind=kOutput, calls=%fused_computation | convolution fusion | flops 151158784 | bytes 8667136 | tf_op jit(solution)/shard_map/while/body/eval_jaxpr/dot_general | solution.py:99
  165.9 7.3 %all-to-all-start = ((bf16[1,16,64,128]{3,1,0,2:T(8,128)(2,1)}), bf16[1,16,64,128]{3,1,0,2:T(8,128)(2,1)S(1)}, u32[]{:S(2)}, u32[]{:S(2)}) async-start(bf16[1,16,64,128]{3,1,0,2:T(8,128)(2,1)} %copy.55), calls=%async_computation | async-start | bytes 524288 | tf_op jit(solution)/shard_map/all_to_all | solution.py:124
  174.9 8.6 %all-to-all-done = bf16[1,16,64,128]{3,1,0,2:T(8,128)(2,1)S(1)} async-done(((bf16[1,16,64,128]{3,1,0,2:T(8,128)(2,1)}), bf16[1,16,64,128]{3,1,0,2:T(8,128)(2,1)S(1)}, u32[]{:S(2)}, u32[]{:S(2)}) %all-to-all-start) | async-done | bytes 262176 | tf_op jit(solution)/shard_map/all_to_all | solution.py:124
  183.5 2.7 %all-to-all-start.1 = ((bf16[1,16,64,128]{3,1,0,2:T(8,128)(2,1)}), bf16[1,16,64,128]{3,1,0,2:T(8,128)(2,1)S(1)}, u32[]{:S(2)}, u32[]{:S(2)}) async-start(bf16[1,16,64,128]{3,1,0,2:T(8,128)(2,1)} %copy.61), calls=%async_computation.1 | async-start | bytes 524288 | tf_op jit(solution)/shard_map/all_to_all | solution.py:125
  186.3 2.3 %reshape.425 = bf16[1,16,2,8,4,8,16]{6,5,4,3,2,1,0:T(8,128)(2,1)} reshape(bf16[1,16,2,32,128]{4,3,2,1,0:T(8,128)(2,1)S(1)} %bitcast.181) | data formatting | bytes 524288 | tf_op jit(solution)/shard_map/reshape | solution.py:117
  188.6 2.7 %copy.57 = bf16[1,16,2,8,8,4,16]{6,5,4,3,2,1,0:T(4,128)(2,1)S(1)} copy(bf16[1,16,2,8,8,4,16]{6,4,5,3,2,1,0:T(8,128)(2,1)} %bitcast.179) | data formatting | bytes 524288 | tf_op jit(solution)/shard_map/transpose | solution.py:120
  191.3 1.1 reshape.426
  192.3 1.4 fusion.52
  193.7 2.6 %all-to-all-done.1 = bf16[1,16,64,128]{3,1,0,2:T(8,128)(2,1)S(1)} async-done(((bf16[1,16,64,128]{3,1,0,2:T(8,128)(2,1)}), bf16[1,16,64,128]{3,1,0,2:T(8,128)(2,1)S(1)}, u32[]{:S(2)}, u32[]{:S(2)}) %all-to-all-start.1) | async-done | bytes 262176 | tf_op jit(solution)/shard_map/all_to_all | solution.py:125
  196.5 2.3 %reshape.427 = bf16[1,16,2,8,4,8,16]{6,5,4,3,2,1,0:T(8,128)(2,1)} reshape(bf16[1,16,2,32,128]{4,3,2,1,0:T(8,128)(2,1)S(1)} %bitcast.182) | data formatting | bytes 524288 | tf_op jit(solution)/shard_map/reshape | solution.py:117
  198.8 2.7 %copy.63 = bf16[1,16,2,8,8,4,16]{6,5,4,3,2,1,0:T(4,128)(2,1)S(1)} copy(bf16[1,16,2,8,8,4,16]{6,4,5,3,2,1,0:T(8,128)(2,1)} %bitcast.180) | data formatting | bytes 524288 | tf_op jit(solution)/shard_map/transpose | solution.py:120
  203.0 1.6 fusion.2
  206.7 1.3 pad_maximum_fusion.3
  (30 shorter events, 9.1 us)
Async XLA Ops:
  124.0 10.1 %slice-start = ((s32[16,8]{0,1:T(8,128)}), s32[16,4]{0,1:T(4,128)S(1)}, s32[]{:S(2)}) async-start(s32[16,8]{0,1:T(8,128)} %param.3), calls=%async_computation.2 | async-start | bytes 4096 | tf_op jit(solution)/shard_map/slice | solution.py:13
  134.3 10.6 %copy-start = (f32[256,8192]{1,0:T(8,128)S(1)}, f32[256,8192]{1,0:T(8,128)}, u32[]{:S(2)}) copy-start(f32[256,8192]{1,0:T(8,128)} %mul.1021) | copy-start | bytes 25165828
  134.3 13.0 %copy-start.1 = (f32[256,8192]{1,0:T(8,128)S(1)}, f32[256,8192]{1,0:T(8,128)}, u32[]{:S(2)}) copy-start(f32[256,8192]{1,0:T(8,128)} %mul.1023) | copy-start | bytes 25165828
  147.3 7.1 %copy-start.2 = (bf16[256,8192]{1,0:T(8,128)(2,1)}, bf16[256,8192]{1,0:T(8,128)(2,1)S(1)}, u32[]{:S(2)}) copy-start(bf16[256,8192]{1,0:T(8,128)(2,1)S(1)} %add_convert_fusion) | copy-start | bytes 12582916
  165.9 17.6 %all-to-all-start = ((bf16[1,16,64,128]{3,1,0,2:T(8,128)(2,1)}), bf16[1,16,64,128]{3,1,0,2:T(8,128)(2,1)S(1)}, u32[]{:S(2)}, u32[]{:S(2)}) async-start(bf16[1,16,64,128]{3,1,0,2:T(8,128)(2,1)} %copy.55), calls=%async_computation | async-start | bytes 524288 | tf_op jit(solution)/shard_map/all_to_all | solution.py:124
  183.5 12.9 %all-to-all-start.1 = ((bf16[1,16,64,128]{3,1,0,2:T(8,128)(2,1)}), bf16[1,16,64,128]{3,1,0,2:T(8,128)(2,1)S(1)}, u32[]{:S(2)}, u32[]{:S(2)}) async-start(bf16[1,16,64,128]{3,1,0,2:T(8,128)(2,1)} %copy.61), calls=%async_computation.1 | async-start | bytes 524288 | tf_op jit(solution)/shard_map/all_to_all | solution.py:125
where the time goes:
time: 210 us; the launch traced here: 208 us
  local copies, waits for them, and re-layouts  100 us (48%)
  other arithmetic  70.8 us (34%)
  matrix products  15.7 us (7%)
  waiting for transfers between devices  11.2 us (5%)
  starting transfers between devices  9.99 us (5%)
    add x1, other arithmetic, spin_products(): total_real + left_real[:, :, None, None] * left_real[None, None]  37.5 us
    another operation x3, other arithmetic  16.3 us
    mul x1, other arithmetic, spin_products(): left_imag[:, :, None, None] * left_real[None, None]  12.5 us
    squeeze x2, local copies, waits for them, and re-layouts, one_slice(): prod_real, prod_imag = spin_products(flattened[0], flattened[1])  11.3 us
    mul x1, local copies, waits for them, and re-layouts, spin_products(): left_real[:, :, None, None] * left_imag[None, None]  10 us
    add x1, local copies, waits for them, and re-layouts, spin_products(): total_real + left_real[:, :, None, None] * left_real[None, None]  10 us
    mul x1, local copies, waits for them, and re-layouts, spin_products(): left_imag[:, :, None, None] * left_real[None, None]  10 us
    mul x1, local copies, waits for them, and re-layouts, spin_products(): left_imag[:, :, None, None] * left_imag[None, None]  10 us
  transfers between devices with their start and end apart: 2, of which 2 were waited for; matrix products, arithmetic and copies ran while one was open for 4% of the time, Pallas kernels for 0%

commit v1 on v0

v1 whole, which is shorter than its diff:
```python
import functools
import math

import jax
import jax.numpy as jnp
import numpy as np
from jax import lax
from jax.experimental import pallas as pl
from jax.experimental.pallas import tpu as pltpu
from jax.sharding import PartitionSpec as P

REMOTE = False
LANES = 128
SPINS = 4
COLORS = 3
PAIRED = 2
MESH = pl.DeviceIdType.MESH


def pair_rows():
    rows = []
    for left in range(SPINS):
        for right in range(left, SPINS):
            for i in range(SPINS):
                for j in range(SPINS):
                    if left == right and i > j:
                        continue
                    if left == right and i == j:
                        rows.append((left, i, right, j, 2))
                    else:
                        rows.append((left, i, right, j, 0))
                        rows.append((left, i, right, j, 1))
    return rows


ROWS = pair_rows()
ROW_OF = {row: position for position, row in enumerate(ROWS)}


def dft_tables(length):
    index = np.arange(length)
    angles = (index[:, None] * index[None, :] % length) * (2.0 * math.pi / length)
    norm = 1.0 / math.sqrt(length)
    half = lambda v: (v * norm).astype(jnp.bfloat16).astype(np.float32)
    return half(np.cos(angles)), half(np.sin(angles))


def table_z(extent):
    cosine, sine = dft_tables(extent)
    per_tile = LANES // extent
    same = np.eye(per_tile, dtype=np.float32)
    block = np.zeros((extent, 2, per_tile, 2, per_tile, extent), np.float32)
    for c_out, c_in, values in ((0, 0, cosine), (0, 1, sine), (1, 0, -sine), (1, 1, cosine)):
        block[:, c_out, :, c_in] = np.einsum("zk,ab->kabz", values, same)
    return block.reshape(2 * LANES, 2 * LANES)


def table_y(extent, local_k):
    cosine, sine = dft_tables(extent)
    per_tile = LANES // extent
    groups = extent // per_tile
    block = np.zeros((groups, local_k, 2, per_tile, 2, local_k, 2, extent), np.float32)
    entries = (
        (0, 0, 0, cosine), (0, 0, 1, sine), (0, 1, 0, -sine), (0, 1, 1, cosine),
        (1, 0, 0, -sine), (1, 0, 1, cosine), (1, 1, 0, -cosine), (1, 1, 1, -sine),
    )
    for copy, c_out, c_in, values in entries:
        for k in range(local_k):
            block[:, k, c_in, :, copy, k, c_out] = values.reshape(groups, per_tile, extent)
    return block.reshape(groups * local_k * 2 * per_tile, 2 * local_k * 2 * extent)


def table_x(extent):
    cosine, sine = dft_tables(extent)
    return np.concatenate([cosine.T, sine.T], axis=1)


def folded_weights(table, rows):
    channels = table.shape[0]
    a1, a2, b1, b2, kind = (rows[i : i + 1, :] for i in range(5))

    def pick(spin, base):
        value = jnp.zeros((channels, rows.shape[1]), jnp.int32)
        for s in range(SPINS):
            value = jnp.where(spin == s, table[:, base + s : base + s + 1], value)
        return value

    def term(l1, l2, r1, r2):
        hit = (pick(r1, 0) == l1) & (pick(l2, 0) == r2)
        code = (pick(r1, SPINS) + pick(l2, SPINS)) & 3
        one = jnp.where(hit, 1.0, 0.0)
        real = jnp.where(code == 0, one, jnp.where(code == 2, -one, 0.0))
        imag = jnp.where(code == 1, one, jnp.where(code == 3, -one, 0.0))
        return real, imag

    fore_real, fore_imag = term(a1, a2, b1, b2)
    back_real, back_imag = term(b1, b2, a1, a2)
    sign = jnp.where(kind == 0, 1.0, jnp.where(kind == 1, -1.0, 0.0))
    real = fore_real + sign * back_real
    imag = fore_imag + sign * back_imag
    weight_real = jnp.where(kind == 1, -imag, real)
    weight_imag = jnp.where(kind == 1, real, imag)
    return jnp.concatenate([weight_real, weight_imag], axis=0).astype(jnp.bfloat16)


def component(s1, c1, s2, c2):
    return ((s1 * COLORS + c1) * SPINS + s2) * COLORS + c2


def products(parts, rows_out):
    def put(row, value):
        rows_out[pl.ds(ROW_OF[row] * 8, 8), :] = value

    colors = [(c1, c2) for c1 in range(COLORS) for c2 in range(COLORS)]
    for left in range(SPINS):
        for right in range(left, SPINS):
            for half in ((0, 1), (2, 3)):
                pairs = [(i, j) for i in half for j in range(SPINS) if left != right or i < j]
                diagonal = half if left == right else ()
                sums = {}
                for c1, c2 in colors:
                    at_a = {i: component(left, c1, i, c2) for i in half}
                    at_b = {j: component(right, c1, j, c2) for j in {j for _, j in pairs}}
                    a = {i: (parts[0, n], parts[1, n], parts[2, n]) for i, n in at_a.items()}
                    b = {j: (parts[0, n], parts[2, n], parts[3, n]) for j, n in at_b.items()}
                    for i, j in pairs:
                        new = (a[i][2] * b[j][0], a[i][0] * b[j][1], a[i][1] * b[j][2])
                        old = sums.get((i, j))
                        sums[i, j] = new if old is None else tuple(o + v for o, v in zip(old, new))
                    for i in diagonal:
                        new = a[i][0] * a[i][0] + a[i][1] * a[i][1]
                        old = sums.get(i)
                        sums[i] = new if old is None else old + new
                for i, j in pairs:
                    first, second, third = sums[i, j]
                    put((left, i, right, j, 0), first - third)
                    put((left, i, right, j, 1), first - second)
                for i in diagonal:
                    put((left, i, right, i, 2), sums[i])


def front_kernel(
    remote, grid_y, prop, table, rows, dft, out,
    staged, parts, prod, dens, weights, sent, load_sems, send_sem, recv_sem,
):
    devices, steps = out.shape[0], out.shape[1]
    tiles = staged.shape[0]
    entries = parts.shape[1]
    channels = table.shape[0]

    def load(t):
        return pltpu.make_async_copy(
            prop.at[:, :, pl.ds(t * LANES, LANES)], staged.at[t], load_sems.at[t]
        )

    for t in range(tiles):
        load(t).start()
    if remote:
        me_x, me_y = lax.axis_index("gx"), lax.axis_index("gy")
        me = me_x * grid_y + me_y
        barrier = pltpu.get_barrier_semaphore()

        @pl.loop(1, devices)
        def _(i):
            to = lax.rem(me + i, devices)
            pl.semaphore_signal(
                barrier, inc=1, device_id={"gx": to // grid_y, "gy": lax.rem(to, grid_y)},
                device_id_type=MESH,
            )

    weights[...] = folded_weights(table[...], rows[...])
    if remote:
        pl.semaphore_wait(barrier, devices - 1)

    @pl.loop(0, steps)
    def _(k):
        @pl.loop(0, PAIRED)
        def _(half):
            t = k * PAIRED + half
            pltpu.make_async_copy(
                prop.at[:, :, pl.ds(0, LANES)], staged.at[t], load_sems.at[t]
            ).wait()
            real = staged[t, 0:entries].astype(jnp.float32)
            parts[0] = real
            imag = staged[t, entries : 2 * entries].astype(jnp.float32)
            parts[1] = imag
            parts[2] = real + imag
            parts[3] = real - imag
            products(parts, prod)
            for x in range(8):
                columns = prod[pl.ds(x, len(ROWS), stride=8), :].astype(jnp.bfloat16)
                value = jnp.dot(weights[...], columns, preferred_element_type=jnp.float32)
                dens[half, 0, pl.ds(x, channels, stride=8), :] = value[:channels]
                dens[half, 1, pl.ds(x, channels, stride=8), :] = value[channels:]

        pieces = []
        for half in range(PAIRED):
            left = jnp.concatenate([dens[half, 0], dens[half, 1]], axis=1).astype(jnp.bfloat16)
            value = lax.dot_general(
                dft[...], left, (((1,), (1,)), ((), ())), preferred_element_type=jnp.float32
            )
            pieces.append(value.reshape(devices, 2 * LANES // devices, LANES))
        block = jnp.concatenate(pieces, axis=1).astype(jnp.bfloat16)
        if not remote:
            out[:, k] = block
        else:
            sent[:, k] = block
            pltpu.make_async_copy(sent.at[me, k], out.at[me, k], recv_sem).start()

            @pl.loop(1, devices)
            def _(i):
                to = lax.rem(me + i, devices)
                pltpu.make_async_remote_copy(
                    src_ref=sent.at[to, k], dst_ref=out.at[me, k],
                    send_sem=send_sem, recv_sem=recv_sem,
                    device_id={"gx": to // grid_y, "gy": lax.rem(to, grid_y)},
                    device_id_type=MESH,
                ).start()

    if remote:
        pltpu.make_async_copy(out, out, recv_sem).wait()
        rest = sent.at[pl.ds(0, devices - 1)]
        pltpu.make_async_copy(rest, rest, send_sem).wait()


def front(prop, gamma_table, devices, grid_y, extent):
    entries, rows_x, sites = prop.shape
    tiles = sites // LANES
    steps = tiles // PAIRED
    height = 2 * LANES // devices * PAIRED
    channels = gamma_table.shape[0]
    rows = np.zeros((8, len(ROWS)), np.int32)
    rows[:5] = np.array(ROWS, np.int32).T
    vmem = pl.BlockSpec(memory_space=pltpu.VMEM)
    return pl.pallas_call(
        functools.partial(front_kernel, REMOTE, grid_y),
        out_shape=jax.ShapeDtypeStruct((devices, steps, height, LANES), jnp.bfloat16),
        in_specs=[pl.BlockSpec(memory_space=pl.ANY), vmem, vmem, vmem],
        out_specs=pl.BlockSpec(memory_space=pl.ANY) if REMOTE else vmem,
        scratch_shapes=[
            pltpu.VMEM((tiles, entries, rows_x, LANES), jnp.bfloat16),
            pltpu.VMEM((4, entries // 2, rows_x, LANES), jnp.float32),
            pltpu.VMEM((len(ROWS) * rows_x, LANES), jnp.float32),
            pltpu.VMEM((PAIRED, 2, channels * rows_x, LANES), jnp.float32),
            pltpu.VMEM((2 * channels, len(ROWS)), jnp.bfloat16),
            pltpu.VMEM((devices, steps, height, LANES), jnp.bfloat16),
            pltpu.SemaphoreType.DMA((tiles,)),
            pltpu.SemaphoreType.DMA,
            pltpu.SemaphoreType.DMA,
        ],
        compiler_params=pltpu.CompilerParams(
            vmem_limit_bytes=40 * 1024 * 1024,
            **(dict(collective_id=0, has_side_effects=True) if REMOTE else {}),
        ),
    )(prop, gamma_table, jnp.asarray(rows), jnp.asarray(table_z(extent), jnp.bfloat16))


def back_kernel(blocks, along_y, along_x, out, mid):
    grid_x, _, width = blocks.shape
    channels, local_k, extent, lanes = out.shape
    rows_x = width // channels
    cols = local_k * lanes
    for gx in range(grid_x):
        mid[gx] = lax.dot_general(
            blocks[gx], along_y[...], (((0,), (0,)), ((), ())), preferred_element_type=jnp.float32
        )
    for g in range(channels):
        value = mid[:, g * rows_x : (g + 1) * rows_x, :].reshape(grid_x * rows_x, 2 * cols)
        value = value.astype(jnp.bfloat16)
        stacked = jnp.concatenate([value[:, :cols], value[:, cols:]], axis=0)
        result = jnp.dot(along_x[...], stacked, preferred_element_type=jnp.float32)
        for k in range(local_k):
            out[g, k] = result[:, k * lanes : (k + 1) * lanes]


def back(blocks, channels, extent, local_k):
    grid_x, _, width = blocks.shape
    vmem = pl.BlockSpec(memory_space=pltpu.VMEM)
    return pl.pallas_call(
        back_kernel,
        out_shape=jax.ShapeDtypeStruct((channels, local_k, extent, 2 * extent), jnp.float32),
        in_specs=[vmem] * 3,
        out_specs=vmem,
        scratch_shapes=[pltpu.VMEM((grid_x, width, 4 * local_k * extent), jnp.float32)],
        compiler_params=pltpu.CompilerParams(vmem_limit_bytes=24 * 1024 * 1024),
    )(
        blocks,
        jnp.asarray(table_y(extent, local_k), jnp.bfloat16),
        jnp.asarray(table_x(extent), jnp.bfloat16),
    )


def body(propagator, gamma_table):
    slices, rows_x, sites = propagator.shape[0], propagator.shape[-2], propagator.shape[-1]
    grid_x, grid_y = lax.axis_size("gx"), lax.axis_size("gy")
    devices = grid_x * grid_y
    extent = grid_x * rows_x
    channels = gamma_table.shape[0]
    local_k = extent // devices
    results = []
    for t in range(slices):
        prop = propagator[t].reshape(-1, rows_x, sites)
        blocks = front(prop, gamma_table, devices, grid_y, extent)
        if not REMOTE:
            blocks = lax.all_to_all(blocks, ("gx", "gy"), split_axis=0, concat_axis=0, tiled=True)
        blocks = blocks.reshape(grid_x, -1, LANES)
        results.append(back(blocks, channels, extent, local_k))
    return jnp.stack(results)


def solution(mesh):
    return jax.shard_map(
        body,
        mesh=mesh,
        in_specs=(P("ta", None, None, None, None, None, "gx", "gy"), P()),
        out_specs=P("ta", None, ("gx", "gy"), None, None),
        check_vma=False,
    )
```

time: 210 us -> 42.1 us (0.20)
  the two profiles are of different devices: /device:TPU:0 before, /device:TPU:1 now
where the time goes in v1:
time: 42.1 us; the launch traced here: 41.8 us
  blocking collectives  22.2 us (53%)
  Pallas kernels  14.9 us (35%)
  local copies, waits for them, and re-layouts  4.7 us (11%)
    all_to_all x1, blocking collectives, body(): lax.all_to_all(blocks, ('gx', 'gy'), split_axis=0, concat_axis=0, tiled=T...  22.2 us
    pallas_call x1, Pallas kernels, front(): pl.pallas_call(functools.partial(front_kernel, REMOTE, grid_y), out_shape...  13.2 us
    unnamed x11, local copies, waits for them, and re-layouts  4.7 us
    pallas_call x1, Pallas kernels, back(): pl.pallas_call(back_kernel, out_shape=jax.ShapeDtypeStruct((channels, loc...  1.7 us

profile of v1, /device:TPU:1, one launch (start us, length us, event | category | flops | bytes accessed | tf_op | source)
XLA Modules:
  0.0 41.8 jit_solution(14071384818075444240)
XLA Ops:
  0.0 0.8 %copy.7.table = s32[16,8]{1,0:T(8,128)S(1)} copy(s32[16,8]{0,1:T(8,128)} %param.7) | data formatting | bytes 1024 | tf_op args[1]
  0.8 0.0 copy-start
  0.8 2.3 %copy-done = bf16[1,2,4,3,4,3,8,1024]{7,6,5,4,3,2,1,0:T(8,128)(2,1)S(1)} copy-done((bf16[1,2,4,3,4,3,8,1024]{7,6,5,4,3,2,1,0:T(8,128)(2,1)S(1)}, bf16[1,2,4,3,4,3,8,1024]{7,6,5,4,3,2,1,0:T(8,128)(2,1)}, u32[]{:S(2)}) %copy-start) | copy-done | bytes 4718616
  3.1 0.0 copy-start.2
  3.1 0.9 %copy-done.2 = bf16[256,256]{1,0:T(8,128)(2,1)S(1)} copy-done((bf16[256,256]{1,0:T(8,128)(2,1)S(1)}, bf16[256,256]{1,0:T(8,128)(2,1)}, u32[]{:S(2)}) %copy-start.2) | copy-done | bytes 131096
  4.0 0.0 copy-start.4
  4.0 0.7 %copy-done.4 = s32[8,256]{1,0:T(8,128)S(1)} copy-done((s32[8,256]{1,0:T(8,128)S(1)}, s32[8,256]{1,0:T(8,128)}, u32[]{:S(2)}) %copy-start.4) | copy-done | bytes 8216
  4.7 0.0 copy-start.1
  4.7 0.0 copy-start.3
  4.7 13.2 %shard_map.64 = bf16[32,4,16,128]{3,2,1,0:T(8,128)(2,1)S(1)} custom-call(bf16[288,8,1024]{2,1,0:T(8,128)(2,1)S(1)} %bitcast.3, s32[16,8]{1,0:T(8,128)S(1)} %copy.7.table, s32[8,256]{1,0:T(8,128)S(1)} %copy-done.4, bf16[256,256]{1,0:T(8,128)(2,1)S(1)} %copy-done.2), custom_call_target="tpu_custom_call" | custom-call | tf_op jit(solution)/shard_map/pallas_call | solution.py:235
  18.0 22.2 %all_to_all.5 = bf16[32,4,16,128]{3,2,1,0:T(8,128)(2,1)S(1)} all-to-all(bf16[32,4,16,128]{3,2,1,0:T(8,128)(2,1)S(1)} %shard_map.64), channel_id=1, replica_groups=mesh['ta'=1,'gx'=8,'gy'=4] {'gx','gy'}, dimensions={0} | all-to-all | bytes 1048576 | tf_op jit(solution)/shard_map/all_to_all | solution.py:305
  40.1 0.0 copy-done.1
  40.1 0.0 copy-done.3
  40.1 1.7 %shard_map.65 = f32[16,2,64,128]{3,2,1,0:T(8,128)} custom-call(bf16[8,256,128]{2,1,0:T(8,128)(2,1)S(1)} %bitcast.4, bf16[256,512]{1,0:T(8,128)(2,1)S(1)} %copy-done.1, bf16[64,128]{1,0:T(8,128)(2,1)S(1)} %copy-done.3), custom_call_target="tpu_custom_call" | custom-call | tf_op jit(solution)/shard_map/pallas_call | solution.py:279
Async XLA Ops:
  0.8 2.3 %copy-start = (bf16[1,2,4,3,4,3,8,1024]{7,6,5,4,3,2,1,0:T(8,128)(2,1)S(1)}, bf16[1,2,4,3,4,3,8,1024]{7,6,5,4,3,2,1,0:T(8,128)(2,1)}, u32[]{:S(2)}) copy-start(bf16[1,2,4,3,4,3,8,1024]{7,6,5,4,3,2,1,0:T(8,128)(2,1)} %param.6) | copy-start | bytes 14155780
  3.1 0.9 %copy-start.2 = (bf16[256,256]{1,0:T(8,128)(2,1)S(1)}, bf16[256,256]{1,0:T(8,128)(2,1)}, u32[]{:S(2)}) copy-start(bf16[256,256]{1,0:T(8,128)(2,1)} %constant.9.clone.dft) | copy-start | bytes 393220
  4.0 0.7 %copy-start.4 = (s32[8,256]{1,0:T(8,128)S(1)}, s32[8,256]{1,0:T(8,128)}, u32[]{:S(2)}) copy-start(s32[8,256]{1,0:T(8,128)} %constant.8.clone.rows) | copy-start | bytes 24580
  4.7 35.4 %copy-start.1 = (bf16[256,512]{1,0:T(8,128)(2,1)S(1)}, bf16[256,512]{1,0:T(8,128)(2,1)}, u32[]{:S(2)}) copy-start(bf16[256,512]{1,0:T(8,128)(2,1)} %constant.10.clone.along_y) | copy-start | bytes 786436
  4.7 35.4 %copy-start.3 = (bf16[64,128]{1,0:T(8,128)(2,1)S(1)}, bf16[64,128]{1,0:T(8,128)(2,1)}, u32[]{:S(2)}) copy-start(bf16[64,128]{1,0:T(8,128)(2,1)} %constant.11.clone.along_x) | copy-start | bytes 49156

commit v2 on v1

--- a/solution.py
+++ b/solution.py
@@ -9,7 +9,7 @@
 from jax.experimental.pallas import tpu as pltpu
 from jax.sharding import PartitionSpec as P
 
-REMOTE = False
+REMOTE = True
 LANES = 128
 SPINS = 4
 COLORS = 3
@@ -249,7 +249,7 @@
             pltpu.SemaphoreType.DMA,
         ],
         compiler_params=pltpu.CompilerParams(
-            vmem_limit_bytes=40 * 1024 * 1024,
+            vmem_limit_bytes=62 * 1024 * 1024,
             **(dict(collective_id=0, has_side_effects=True) if REMOTE else {}),
         ),
     )(prop, gamma_table, jnp.asarray(rows), jnp.asarray(table_z(extent), jnp.bfloat16))

time: 42.1 us -> 30.6 us (0.73)
  the two profiles are of different devices: /device:TPU:1 before, /device:TPU:0 now
where the time goes in v2:
time: 30.6 us; the launch traced here: 30.4 us
  Pallas kernels  28 us (92%)
  local copies, waits for them, and re-layouts  2.44 us (8%)
    pallas_call x1, Pallas kernels, front(): pl.pallas_call(functools.partial(front_kernel, REMOTE, grid_y), out_shape...  26.3 us
    unnamed x7, local copies, waits for them, and re-layouts  2.44 us
    pallas_call x1, Pallas kernels, back(): pl.pallas_call(back_kernel, out_shape=jax.ShapeDtypeStruct((channels, loc...  1.7 us

profile of v2, /device:TPU:0, one launch (start us, length us, event | category | flops | bytes accessed | tf_op | source)
XLA Modules:
  0.0 30.4 jit_solution(3931174997899292458)
XLA Ops:
  0.0 0.0 copy-start.2
  0.0 0.0 copy-start.1
  0.0 1.4 %copy.7.table = s32[16,8]{1,0:T(8,128)} copy(s32[16,8]{0,1:T(8,128)} %param.7) | data formatting | bytes 1024 | tf_op args[1]
  1.4 26.3 %shard_map.64 = bf16[32,4,16,128]{3,2,1,0:T(8,128)(2,1)} custom-call(bf16[288,8,1024]{2,1,0:T(8,128)(2,1)} %bitcast.4, s32[16,8]{1,0:T(8,128)} %copy.7.table, s32[8,256]{1,0:T(8,128)} %constant.8.clone.rows, bf16[256,256]{1,0:T(8,128)(2,1)} %constant.9.clone.dft), custom_call_target="tpu_custom_call" | custom-call | tf_op jit(solution)/shard_map/pallas_call | solution.py:235
  27.7 0.0 copy-done.2
  27.7 0.0 copy-done.1
  27.7 0.0 copy-start
  27.7 1.0 %copy-done = bf16[32,4,16,128]{3,2,1,0:T(8,128)(2,1)S(1)} copy-done((bf16[32,4,16,128]{3,2,1,0:T(8,128)(2,1)S(1)}, bf16[32,4,16,128]{3,2,1,0:T(8,128)(2,1)}, u32[]{:S(2)}) %copy-start) | copy-done | bytes 524312
  28.7 1.7 %shard_map.65 = f32[16,2,64,128]{3,2,1,0:T(8,128)} custom-call(bf16[8,256,128]{2,1,0:T(8,128)(2,1)S(1)} %bitcast.3, bf16[256,512]{1,0:T(8,128)(2,1)S(1)} %copy-done.1, bf16[64,128]{1,0:T(8,128)(2,1)S(1)} %copy-done.2), custom_call_target="tpu_custom_call" | custom-call | tf_op jit(solution)/shard_map/pallas_call | solution.py:279
Async XLA Ops:
  0.0 27.7 %copy-start.2 = (bf16[64,128]{1,0:T(8,128)(2,1)S(1)}, bf16[64,128]{1,0:T(8,128)(2,1)}, u32[]{:S(2)}) copy-start(bf16[64,128]{1,0:T(8,128)(2,1)} %constant.11.clone.along_x) | copy-start | bytes 49156
  0.0 27.7 %copy-start.1 = (bf16[256,512]{1,0:T(8,128)(2,1)S(1)}, bf16[256,512]{1,0:T(8,128)(2,1)}, u32[]{:S(2)}) copy-start(bf16[256,512]{1,0:T(8,128)(2,1)} %constant.10.clone.along_y) | copy-start | bytes 786436
  27.7 1.0 %copy-start = (bf16[32,4,16,128]{3,2,1,0:T(8,128)(2,1)S(1)}, bf16[32,4,16,128]{3,2,1,0:T(8,128)(2,1)}, u32[]{:S(2)}) copy-start(bf16[32,4,16,128]{3,2,1,0:T(8,128)(2,1)} %shard_map.64) | copy-start | bytes 1572868

commit v3 on v2

--- a/solution.py
+++ b/solution.py
@@ -9,11 +9,10 @@
 from jax.experimental.pallas import tpu as pltpu
 from jax.sharding import PartitionSpec as P
 
-REMOTE = True
 LANES = 128
 SPINS = 4
 COLORS = 3
-PAIRED = 2
+PAIRED = 1
 MESH = pl.DeviceIdType.MESH
 
 
@@ -140,37 +139,58 @@
 
 
 def front_kernel(
-    remote, grid_y, prop, table, rows, dft, out,
-    staged, parts, prod, dens, weights, sent, load_sems, send_sem, recv_sem,
+    grid_x, grid_y, prop, table_in, rows_in, dft_in, out,
+    staged, parts, prod, dens, weights, sent, table, rows, dft,
+    load_sems, small_sems, send_sem, recv_sem,
 ):
     devices, steps = out.shape[0], out.shape[1]
     tiles = staged.shape[0]
     entries = parts.shape[1]
-    channels = table.shape[0]
+    channels = table.shape[1]
 
     def load(t):
         return pltpu.make_async_copy(
             prop.at[:, :, pl.ds(t * LANES, LANES)], staged.at[t], load_sems.at[t]
         )
 
-    for t in range(tiles):
+    me_x, me_y = lax.axis_index("gx"), lax.axis_index("gy")
+    me = me_x * grid_y + me_y
+    if grid_y == 4:
+        columns_y = [lax.rem(me_y + 2, 4), 3 - me_y, me_y + 1 - 2 * lax.rem(me_y, 2)]
+    else:
+        columns_y = [lax.rem(me_y + i, grid_y) for i in range(1, grid_y)]
+
+    def for_others(act):
+        @pl.loop(0, grid_x)
+        def _(i):
+            to_x = lax.rem(me_x + i, grid_x)
+            for to_y in columns_y:
+                act(to_x, to_y)
+
+        @pl.loop(1, grid_x)
+        def _(i):
+            act(lax.rem(me_x + i, grid_x), me_y)
+
+    small = [
+        pltpu.make_async_copy(source, target, small_sems.at[n])
+        for n, (source, target) in enumerate(((table_in, table), (rows_in, rows), (dft_in, dft)))
+    ]
+    load(0).start()
+    for copy in small:
+        copy.start()
+    for t in range(1, tiles):
         load(t).start()
-    if remote:
-        me_x, me_y = lax.axis_index("gx"), lax.axis_index("gy")
-        me = me_x * grid_y + me_y
-        barrier = pltpu.get_barrier_semaphore()
-
-        @pl.loop(1, devices)
-        def _(i):
-            to = lax.rem(me + i, devices)
-            pl.semaphore_signal(
-                barrier, inc=1, device_id={"gx": to // grid_y, "gy": lax.rem(to, grid_y)},
-                device_id_type=MESH,
-            )
-
-    weights[...] = folded_weights(table[...], rows[...])
-    if remote:
-        pl.semaphore_wait(barrier, devices - 1)
+    barrier = pltpu.get_barrier_semaphore()
+    for_others(
+        lambda x, y: pl.semaphore_signal(
+            barrier, inc=1, device_id={"gx": x, "gy": y}, device_id_type=MESH
+        )
+    )
+    small[0].wait()
+    small[1].wait()
+    weights[...] = folded_weights(jnp.transpose(table[...]), rows[...])
+    small[2].wait()
+    pl.semaphore_wait(barrier, grid_x * grid_y - 1)
 
     @pl.loop(0, steps)
     def _(k):
@@ -201,26 +221,19 @@
             )
             pieces.append(value.reshape(devices, 2 * LANES // devices, LANES))
         block = jnp.concatenate(pieces, axis=1).astype(jnp.bfloat16)
-        if not remote:
-            out[:, k] = block
-        else:
-            sent[:, k] = block
-            pltpu.make_async_copy(sent.at[me, k], out.at[me, k], recv_sem).start()
-
-            @pl.loop(1, devices)
-            def _(i):
-                to = lax.rem(me + i, devices)
-                pltpu.make_async_remote_copy(
-                    src_ref=sent.at[to, k], dst_ref=out.at[me, k],
-                    send_sem=send_sem, recv_sem=recv_sem,
-                    device_id={"gx": to // grid_y, "gy": lax.rem(to, grid_y)},
-                    device_id_type=MESH,
-                ).start()
-
-    if remote:
-        pltpu.make_async_copy(out, out, recv_sem).wait()
-        rest = sent.at[pl.ds(0, devices - 1)]
-        pltpu.make_async_copy(rest, rest, send_sem).wait()
+        sent[:, k] = block
+        pltpu.make_async_copy(sent.at[me, k], out.at[me, k], recv_sem).start()
+        for_others(
+            lambda x, y: pltpu.make_async_remote_copy(
+                src_ref=sent.at[x * grid_y + y, k], dst_ref=out.at[me, k],
+                send_sem=send_sem, recv_sem=recv_sem,
+                device_id={"gx": x, "gy": y}, device_id_type=MESH,
+            ).start()
+        )
+
+    pltpu.make_async_copy(out, out, recv_sem).wait()
+    rest = sent.at[pl.ds(0, devices - 1)]
+    pltpu.make_async_copy(rest, rest, send_sem).wait()
 
 
 def front(prop, gamma_table, devices, grid_y, extent):
@@ -231,12 +244,11 @@
     channels = gamma_table.shape[0]
     rows = np.zeros((8, len(ROWS)), np.int32)
     rows[:5] = np.array(ROWS, np.int32).T
-    vmem = pl.BlockSpec(memory_space=pltpu.VMEM)
     return pl.pallas_call(
-        functools.partial(front_kernel, REMOTE, grid_y),
+        functools.partial(front_kernel, devices // grid_y, grid_y),
         out_shape=jax.ShapeDtypeStruct((devices, steps, height, LANES), jnp.bfloat16),
-        in_specs=[pl.BlockSpec(memory_space=pl.ANY), vmem, vmem, vmem],
-        out_specs=pl.BlockSpec(memory_space=pl.ANY) if REMOTE else vmem,
+        in_specs=[pl.BlockSpec(memory_space=pl.ANY)] * 4,
+        out_specs=pl.BlockSpec(memory_space=pl.ANY),
         scratch_shapes=[
             pltpu.VMEM((tiles, entries, rows_x, LANES), jnp.bfloat16),
             pltpu.VMEM((4, entries // 2, rows_x, LANES), jnp.float32),
@@ -244,23 +256,33 @@
             pltpu.VMEM((PAIRED, 2, channels * rows_x, LANES), jnp.float32),
             pltpu.VMEM((2 * channels, len(ROWS)), jnp.bfloat16),
             pltpu.VMEM((devices, steps, height, LANES), jnp.bfloat16),
+            pltpu.VMEM(gamma_table.shape[::-1], jnp.int32),
+            pltpu.VMEM(rows.shape, jnp.int32),
+            pltpu.VMEM((2 * LANES, 2 * LANES), jnp.bfloat16),
             pltpu.SemaphoreType.DMA((tiles,)),
+            pltpu.SemaphoreType.DMA((3,)),
             pltpu.SemaphoreType.DMA,
             pltpu.SemaphoreType.DMA,
         ],
         compiler_params=pltpu.CompilerParams(
-            vmem_limit_bytes=62 * 1024 * 1024,
-            **(dict(collective_id=0, has_side_effects=True) if REMOTE else {}),
+            vmem_limit_bytes=62 * 1024 * 1024, collective_id=0, has_side_effects=True
         ),
-    )(prop, gamma_table, jnp.asarray(rows), jnp.asarray(table_z(extent), jnp.bfloat16))
-
-
-def back_kernel(blocks, along_y, along_x, out, mid):
+    )(prop, gamma_table.T, jnp.asarray(rows), jnp.asarray(table_z(extent), jnp.bfloat16))
+
+
+def back_kernel(blocks_in, along_y, along_x, out, blocks, mid, sems):
     grid_x, _, width = blocks.shape
+    copies = [
+        pltpu.make_async_copy(blocks_in.at[gx], blocks.at[gx], sems.at[gx])
+        for gx in range(grid_x)
+    ]
+    for copy in copies:
+        copy.start()
     channels, local_k, extent, lanes = out.shape
     rows_x = width // channels
     cols = local_k * lanes
     for gx in range(grid_x):
+        copies[gx].wait()
         mid[gx] = lax.dot_general(
             blocks[gx], along_y[...], (((0,), (0,)), ((), ())), preferred_element_type=jnp.float32
         )
@@ -279,10 +301,14 @@
     return pl.pallas_call(
         back_kernel,
         out_shape=jax.ShapeDtypeStruct((channels, local_k, extent, 2 * extent), jnp.float32),
-        in_specs=[vmem] * 3,
+        in_specs=[pl.BlockSpec(memory_space=pl.ANY), vmem, vmem],
         out_specs=vmem,
-        scratch_shapes=[pltpu.VMEM((grid_x, width, 4 * local_k * extent), jnp.float32)],
-        compiler_params=pltpu.CompilerParams(vmem_limit_bytes=24 * 1024 * 1024),
+        scratch_shapes=[
+            pltpu.VMEM(blocks.shape, blocks.dtype),
+            pltpu.VMEM((grid_x, width, 4 * local_k * extent), jnp.float32),
+            pltpu.SemaphoreType.DMA((grid_x,)),
+        ],
+        compiler_params=pltpu.CompilerParams(vmem_limit_bytes=62 * 1024 * 1024),
     )(
         blocks,
         jnp.asarray(table_y(extent, local_k), jnp.bfloat16),
@@ -301,8 +327,6 @@
     for t in range(slices):
         prop = propagator[t].reshape(-1, rows_x, sites)
         blocks = front(prop, gamma_table, devices, grid_y, extent)
-        if not REMOTE:
-            blocks = lax.all_to_all(blocks, ("gx", "gy"), split_axis=0, concat_axis=0, tiled=True)
         blocks = blocks.reshape(grid_x, -1, LANES)
         results.append(back(blocks, channels, extent, local_k))
     return jnp.stack(results)

time: 30.6 us -> 31.1 us (1.016)
  Pallas kernels: 28 us -> 30.9 us
  local copies, waits for them, and re-layouts: 2.44 us -> 0 us
    pallas_call x1, Pallas kernels: 1.7 us -> 4.78 us  [back(): pl.pallas_call(back_kernel, out_shape=jax.ShapeDtypeStruct((channels, loc...]
    unnamed x7 -> x0, local copies, waits for them, and re-layouts: 2.44 us -> none
where the time goes in v3:
time: 31.1 us; the launch traced here: 30.9 us
  Pallas kernels  30.9 us (99%)
    pallas_call x1, Pallas kernels, front(): pl.pallas_call(functools.partial(front_kernel, devices // grid_y, grid_y)...  26.1 us
    pallas_call x1, Pallas kernels, back(): pl.pallas_call(back_kernel, out_shape=jax.ShapeDtypeStruct((channels, loc...  4.78 us

profile of v3, /device:TPU:0, one launch (start us, length us, event | category | flops | bytes accessed | tf_op | source)
XLA Modules:
  0.0 30.9 jit_solution(13596476130146085074)
XLA Ops:
  0.0 26.1 %shard_map.64 = bf16[32,8,8,128]{3,2,1,0:T(8,128)(2,1)} custom-call(bf16[288,8,1024]{2,1,0:T(8,128)(2,1)} %bitcast.4, s32[8,16]{1,0:T(8,128)} %bitcast.6, s32[8,256]{1,0:T(8,128)} %constant.8.clone.rows_in, bf16[256,256]{1,0:T(8,128)(2,1)} %constant.9.clone.dft_in), custom_call_target="tpu_custom_call" | custom-call | tf_op jit(solution)/shard_map/pallas_call | solution.py:247
  26.1 4.8 %shard_map.65 = f32[16,2,64,128]{3,2,1,0:T(8,128)} custom-call(bf16[8,256,128]{2,1,0:T(8,128)(2,1)} %bitcast.5, bf16[256,512]{1,0:T(8,128)(2,1)} %constant.10.clone.along_y, bf16[64,128]{1,0:T(8,128)(2,1)} %constant.11.clone.along_x), custom_call_target="tpu_custom_call" | custom-call | tf_op jit(solution)/shard_map/pallas_call | solution.py:301

commit v4 on v3

--- a/solution.py
+++ b/solution.py
@@ -12,7 +12,7 @@
 LANES = 128
 SPINS = 4
 COLORS = 3
-PAIRED = 1
+PAIRED = 2
 MESH = pl.DeviceIdType.MESH
 
 
@@ -156,20 +156,20 @@
     me_x, me_y = lax.axis_index("gx"), lax.axis_index("gy")
     me = me_x * grid_y + me_y
     if grid_y == 4:
-        columns_y = [lax.rem(me_y + 2, 4), 3 - me_y, me_y + 1 - 2 * lax.rem(me_y, 2)]
+        columns_y = [lax.rem(me_y + 2, 4), me_y + 1 - 2 * lax.rem(me_y, 2), 3 - me_y]
     else:
         columns_y = [lax.rem(me_y + i, grid_y) for i in range(1, grid_y)]
 
     def for_others(act):
-        @pl.loop(0, grid_x)
+        @pl.loop(1, grid_x)
         def _(i):
             to_x = lax.rem(me_x + i, grid_x)
             for to_y in columns_y:
                 act(to_x, to_y)
-
-        @pl.loop(1, grid_x)
-        def _(i):
-            act(lax.rem(me_x + i, grid_x), me_y)
+            act(to_x, me_y)
+
+        for to_y in columns_y:
+            act(me_x, to_y)
 
     small = [
         pltpu.make_async_copy(source, target, small_sems.at[n])
@@ -270,19 +270,12 @@
     )(prop, gamma_table.T, jnp.asarray(rows), jnp.asarray(table_z(extent), jnp.bfloat16))
 
 
-def back_kernel(blocks_in, along_y, along_x, out, blocks, mid, sems):
+def back_kernel(blocks, along_y, along_x, out, mid):
     grid_x, _, width = blocks.shape
-    copies = [
-        pltpu.make_async_copy(blocks_in.at[gx], blocks.at[gx], sems.at[gx])
-        for gx in range(grid_x)
-    ]
-    for copy in copies:
-        copy.start()
     channels, local_k, extent, lanes = out.shape
     rows_x = width // channels
     cols = local_k * lanes
     for gx in range(grid_x):
-        copies[gx].wait()
         mid[gx] = lax.dot_general(
             blocks[gx], along_y[...], (((0,), (0,)), ((), ())), preferred_element_type=jnp.float32
         )
@@ -301,14 +294,10 @@
     return pl.pallas_call(
         back_kernel,
         out_shape=jax.ShapeDtypeStruct((channels, local_k, extent, 2 * extent), jnp.float32),
-        in_specs=[pl.BlockSpec(memory_space=pl.ANY), vmem, vmem],
+        in_specs=[vmem] * 3,
         out_specs=vmem,
-        scratch_shapes=[
-            pltpu.VMEM(blocks.shape, blocks.dtype),
-            pltpu.VMEM((grid_x, width, 4 * local_k * extent), jnp.float32),
-            pltpu.SemaphoreType.DMA((grid_x,)),
-        ],
-        compiler_params=pltpu.CompilerParams(vmem_limit_bytes=62 * 1024 * 1024),
+        scratch_shapes=[pltpu.VMEM((grid_x, width, 4 * local_k * extent), jnp.float32)],
+        compiler_params=pltpu.CompilerParams(vmem_limit_bytes=24 * 1024 * 1024),
     )(
         blocks,
         jnp.asarray(table_y(extent, local_k), jnp.bfloat16),

time: 31.1 us -> 27.3 us (0.88)
  Pallas kernels: 30.9 us -> 26.1 us
  local copies, waits for them, and re-layouts: 0 us -> 1.04 us
    pallas_call x1, Pallas kernels: 4.78 us -> 1.7 us  [back(): pl.pallas_call(back_kernel, out_shape=jax.ShapeDtypeStruct((channels, loc...]
    pallas_call x1, Pallas kernels: 26.1 us -> 24.4 us  [front(): pl.pallas_call(functools.partial(front_kernel, devices // grid_y, grid_y)...]
    unnamed x0 -> x6, local copies, waits for them, and re-layouts: none -> 1.04 us
where the time goes in v4:
time: 27.3 us; the launch traced here: 27.2 us
  Pallas kernels  26.1 us (96%)
  local copies, waits for them, and re-layouts  1.04 us (4%)
    pallas_call x1, Pallas kernels, front(): pl.pallas_call(functools.partial(front_kernel, devices // grid_y, grid_y)...  24.4 us
    pallas_call x1, Pallas kernels, back(): pl.pallas_call(back_kernel, out_shape=jax.ShapeDtypeStruct((channels, loc...  1.7 us
    unnamed x6, local copies, waits for them, and re-layouts  1.04 us

profile of v4, /device:TPU:0, one launch (start us, length us, event | category | flops | bytes accessed | tf_op | source)
XLA Modules:
  0.0 27.2 jit_solution(12451069999415516251)
XLA Ops:
  0.0 0.0 copy-start.2
  0.0 0.0 copy-start.1
  0.0 24.4 %shard_map.64 = bf16[32,4,16,128]{3,2,1,0:T(8,128)(2,1)} custom-call(bf16[288,8,1024]{2,1,0:T(8,128)(2,1)} %bitcast.5, s32[8,16]{1,0:T(8,128)} %bitcast.6, s32[8,256]{1,0:T(8,128)} %constant.8.clone.rows_in, bf16[256,256]{1,0:T(8,128)(2,1)} %constant.9.clone.dft_in), custom_call_target="tpu_custom_call" | custom-call | tf_op jit(solution)/shard_map/pallas_call | solution.py:247
  24.4 0.0 copy-done.2
  24.4 0.0 copy-done.1
  24.4 0.0 copy-start
  24.5 1.0 %copy-done = bf16[32,4,16,128]{3,2,1,0:T(8,128)(2,1)S(1)} copy-done((bf16[32,4,16,128]{3,2,1,0:T(8,128)(2,1)S(1)}, bf16[32,4,16,128]{3,2,1,0:T(8,128)(2,1)}, u32[]{:S(2)}) %copy-start) | copy-done | bytes 524312
  25.5 1.7 %shard_map.65 = f32[16,2,64,128]{3,2,1,0:T(8,128)} custom-call(bf16[8,256,128]{2,1,0:T(8,128)(2,1)S(1)} %bitcast.4, bf16[256,512]{1,0:T(8,128)(2,1)S(1)} %copy-done.1, bf16[64,128]{1,0:T(8,128)(2,1)S(1)} %copy-done.2), custom_call_target="tpu_custom_call" | custom-call | tf_op jit(solution)/shard_map/pallas_call | solution.py:294
Async XLA Ops:
  0.0 24.4 %copy-start.2 = (bf16[64,128]{1,0:T(8,128)(2,1)S(1)}, bf16[64,128]{1,0:T(8,128)(2,1)}, u32[]{:S(2)}) copy-start(bf16[64,128]{1,0:T(8,128)(2,1)} %constant.11.clone.along_x) | copy-start | bytes 49156
  0.0 24.4 %copy-start.1 = (bf16[256,512]{1,0:T(8,128)(2,1)S(1)}, bf16[256,512]{1,0:T(8,128)(2,1)}, u32[]{:S(2)}) copy-start(bf16[256,512]{1,0:T(8,128)(2,1)} %constant.10.clone.along_y) | copy-start | bytes 786436
  24.4 1.0 %copy-start = (bf16[32,4,16,128]{3,2,1,0:T(8,128)(2,1)S(1)}, bf16[32,4,16,128]{3,2,1,0:T(8,128)(2,1)}, u32[]{:S(2)}) copy-start(bf16[32,4,16,128]{3,2,1,0:T(8,128)(2,1)} %shard_map.64) | copy-start | bytes 1572868
